TPU v7x, 512 devices: a 8x2x16 block of a 8x8x16 slice. The times are simulated.
512 devices in a mesh: grp: 2 (over y), seq: 16 (over z), head: 8 (over x), sub: 2 (over core).
Axes of the slice: x: 8, y: 2, z: 16, core: 2. Of those that a mesh axis runs over, the one named last changes fastest.
The devices are a block of a 8x8x16 slice.
Arguments:
- vid_q: bfloat16 [10240, 4096], P(('grp', 'seq', 'sub'), 'head'), parts along dimension 0, may hold values from -6 to 6
- vid_k: bfloat16 [10240, 4096], P(('grp', 'seq', 'sub'), 'head'), parts along dimension 0, may hold values from -6 to 6
- vid_v: bfloat16 [10240, 4096], P(('grp', 'seq', 'sub'), 'head'), parts along dimension 0, may hold values from -6 to 6
- aud_q: bfloat16 [2560, 2048], P(('grp', 'seq', 'sub'), 'head'), parts along dimension 0, may hold values from -6 to 6
- cross_k: bfloat16 [10240, 2048], P(('grp', 'seq', 'sub'), 'head'), parts along dimension 0, may hold values from -6 to 6
- cross_v: bfloat16 [10240, 2048], P(('grp', 'seq', 'sub'), 'head'), parts along dimension 0, may hold values from -6 to 6
- cross_q: bfloat16 [10240, 2048], P(('grp', 'seq', 'sub'), 'head'), parts along dimension 0, may hold values from -6 to 6
- aud_k: bfloat16 [2560, 2048], P(('grp', 'seq', 'sub'), 'head'), parts along dimension 0, may hold values from -6 to 6
- aud_v: bfloat16 [2560, 2048], P(('grp', 'seq', 'sub'), 'head'), parts along dimension 0, may hold values from -6 to 6
- windows: int32 [2, 320], P(None, 'grp'), parts along dimension 1, may hold values from 0 to 160, as said below
Outputs:
- video_self: bfloat16 [10240, 4096], P(('grp', 'seq', 'sub'), 'head'), parts along dimension 0
- audio_out: bfloat16 [2560, 2048], P(('grp', 'seq', 'sub'), 'head'), parts along dimension 0
- video_cross: bfloat16 [10240, 2048], P(('grp', 'seq', 'sub'), 'head'), parts along dimension 0
There are 2 independent parts, one for each index of `grp`. A program takes and returns all parts, laid end to end along the dimension named above; each array names one. Nothing has to cross between parts.
Inputs may be any that keep to these rules, and one draw needn't show every extreme that they name: For every stretch c, windows[0, c] lies between max(0, c - 5) and c, and windows[1, c] between c + 1 and min(160, c + 6); in every draw some stretch reaches 5 tiles on both sides.
All inputs are finite; a program needn't handle non-finite values.
Results may differ from a plain program's by a relative error of at most 0.03.
Values may be sent and summed in bfloat16 or wider, within the bound.
No kernel may reach another device: no remote copies, remote signals or barrier semaphores. Data moves between devices by JAX's collectives and lax.ppermute only.
A program may use at most 64 MiB of HBM per device.

v0:
```python
from functools import partial
import math
import jax
import jax.numpy as jnp
from jax import lax
from jax.sharding import PartitionSpec as P

HEAD_DIM = 128
AUDIO_DIM = 64
TILE_LEN = 32
STRETCH_LEN = 8


def with_halo(array, sides, width):
    edges = {}
    for axis, dim in sides:
        count, length = (lax.axis_size(axis), array.shape[dim])
        up = [(i, (i + 1) % count) for i in range(count - 1)]
        last = lax.slice_in_dim(array, length - width, length, axis=dim)
        leading = lax.slice_in_dim(array, 0, width, axis=dim)
        edges[dim] = (
            lax.ppermute(last, axis, up),
            lax.ppermute(leading, axis, [(b, a) for a, b in up]),
        )
    done = []
    for _, dim in sides:
        low, high = edges[dim]
        around = [(width, width) if d in done else (0, 0) for d in range(array.ndim)]
        array = jnp.concatenate([jnp.pad(low, around), array, jnp.pad(high, around)], axis=dim)
        done.append(dim)
    return array


def start_state(query_count, head_count, head_size):
    running = jnp.full((head_count, query_count), -jnp.inf, jnp.float32)
    summed = jnp.zeros((head_count, query_count), jnp.float32)
    numerator = jnp.zeros((head_count, query_count, head_size), jnp.float32)
    return (running, summed, numerator)


def absorb(state_in, queries, key_rows, value_rows, head_count, scaling, visible):
    running, summed, numerator = state_in
    query_count = queries.shape[0]
    key_count = key_rows.shape[0]
    head_size = queries.shape[1] // head_count
    scores = (
        jnp.einsum(
            "qhe,khe->hqk",
            queries.reshape(query_count, head_count, head_size),
            key_rows.reshape(key_count, head_count, head_size),
            preferred_element_type=jnp.float32,
        )
        * scaling
    )
    if visible is not None:
        scores = jnp.where(visible[None], scores, jnp.float32(-1e30))
    newest = jnp.maximum(running, jnp.max(scores, axis=2))
    shrink = jnp.exp(running - newest)
    weights = jnp.exp(scores - newest[:, :, None])
    summed = summed * shrink + jnp.sum(weights, axis=2)
    numerator = numerator * shrink[:, :, None] + jnp.einsum(
        "hqk,khe->hqe",
        weights.astype(jnp.bfloat16),
        value_rows.reshape(key_count, head_count, head_size),
        preferred_element_type=jnp.float32,
    )
    return (newest, summed, numerator)


def block_split(total_rows):
    block_rows = total_rows
    while block_rows > 512 and block_rows % 2 == 0:
        block_rows = block_rows // 2
    return (block_rows, total_rows // block_rows)


def fold_joint(
    states_in,
    combined,
    offset,
    video_queries,
    audio_queries,
    video_heads,
    audio_heads,
    video_scaling,
    audio_scaling,
):
    video_width = video_queries.shape[1]
    audio_width = audio_queries.shape[1]
    block_rows, block_count = block_split(combined.shape[0])
    blocks = combined.reshape(block_count, block_rows, combined.shape[1])

    def one_block(states, rows):
        video_state = absorb(
            states[0],
            video_queries,
            rows[:, :video_width],
            rows[:, video_width : 2 * video_width],
            video_heads,
            video_scaling,
            None,
        )
        audio_state = absorb(
            states[1],
            audio_queries,
            rows[:, 2 * video_width : 2 * video_width + audio_width],
            rows[:, 2 * video_width + audio_width :],
            audio_heads,
            audio_scaling,
            None,
        )
        return ((video_state, audio_state), None)

    result, unused = lax.scan(one_block, states_in, blocks)
    return result


def normalize_heads(state_in):
    running, summed, numerator = state_in
    mixed = numerator / summed[:, :, None]
    return mixed.transpose(1, 0, 2).reshape(mixed.shape[1], -1).astype(jnp.bfloat16)


def body(vid_q, vid_k, vid_v, aud_q, cross_k, cross_v, cross_q, aud_k, aud_v, windows):
    video_heads = vid_q.shape[1] // HEAD_DIM
    video_scaling = 1.0 / math.sqrt(HEAD_DIM)
    audio_heads = aud_q.shape[1] // AUDIO_DIM
    audio_scaling = 1.0 / math.sqrt(AUDIO_DIM)
    combined = jnp.concatenate((vid_k, vid_v, cross_k, cross_v), axis=1)
    folder = partial(
        fold_joint,
        video_queries=vid_q,
        audio_queries=aud_q,
        video_heads=video_heads,
        audio_heads=audio_heads,
        video_scaling=video_scaling,
        audio_scaling=audio_scaling,
    )
    initial = (
        start_state(vid_q.shape[0], video_heads, HEAD_DIM),
        start_state(aud_q.shape[0], audio_heads, AUDIO_DIM),
    )
    video_state, audio_state = folder(
        initial, lax.all_gather(combined, ("seq", "sub"), axis=0, tiled=True), jnp.int32(0)
    )
    video_self = normalize_heads(video_state)
    audio_out = normalize_heads(audio_state)
    audio_rows = aud_k.shape[0]
    key_width = aud_k.shape[1]
    padded_rows = with_halo(
        jnp.concatenate((aud_k, aud_v), axis=1), ((("seq", "sub"), 0),), audio_rows
    )
    near_keys = padded_rows[:, :key_width]
    near_values = padded_rows[:, key_width:]
    position = lax.axis_index(("seq", "sub"))
    audio_index = (position - 1) * audio_rows + jnp.arange(padded_rows.shape[0], dtype=jnp.int32)
    stretch_index = audio_index // STRETCH_LEN
    stretch_ids = jnp.arange(windows.shape[1], dtype=jnp.int32)
    onehot = stretch_index[:, None] == stretch_ids[None, :]
    first_tile = jnp.sum(jnp.where(onehot, windows[0][None, :], 0), axis=1)
    after_tile = jnp.sum(jnp.where(onehot, windows[1][None, :], 0), axis=1)
    video_rows = cross_q.shape[0]
    video_tile = (position * video_rows + jnp.arange(video_rows, dtype=jnp.int32)) // TILE_LEN
    visible = (first_tile[None, :] <= video_tile[:, None]) & (
        video_tile[:, None] < after_tile[None, :]
    )
    state = absorb(
        start_state(video_rows, audio_heads, AUDIO_DIM),
        cross_q,
        near_keys,
        near_values,
        audio_heads,
        audio_scaling,
        visible,
    )
    video_cross = normalize_heads(state)
    return (video_self, audio_out, video_cross)


def solution(mesh):
    return jax.shard_map(
        body,
        mesh=mesh,
        in_specs=(
            P(("grp", "seq", "sub"), "head"),
            P(("grp", "seq", "sub"), "head"),
            P(("grp", "seq", "sub"), "head"),
            P(("grp", "seq", "sub"), "head"),
            P(("grp", "seq", "sub"), "head"),
            P(("grp", "seq", "sub"), "head"),
            P(("grp", "seq", "sub"), "head"),
            P(("grp", "seq", "sub"), "head"),
            P(("grp", "seq", "sub"), "head"),
            P(None, "grp"),
        ),
        out_specs=(
            P(("grp", "seq", "sub"), "head"),
            P(("grp", "seq", "sub"), "head"),
            P(("grp", "seq", "sub"), "head"),
        ),
        check_vma=False,
    )
```

profile of v0, /device:TPU:65, one launch (start us, length us, event | category | flops | bytes accessed | tf_op | source)
XLA Modules:
  0.0 245.9 jit_solution(11769549434553629268)
XLA Ops:
  7.2 1.9 pad_maximum_fusion
  9.2 0.7 constant_dynamic-update-slice_fusion.1
  9.9 0.7 constant_dynamic-update-slice_fusion
  10.7 7.0 %collective-permute-start = (bf16[40,512]{1,0:T(8,128)(2,1)S(1)}, bf16[40,512]{1,0:T(8,128)(2,1)S(1)}, u32[]{:S(2)}, u32[]{:S(2)}) collective-permute-start(bf16[40,512]{1,0:T(8,128)(2,1)S(1)} %constant_dynamic-update-slice_fusion), channel_id=1, source_target_pairs={{0,1},{1,16},{16,17},{17,32},{32,33},{33,48},{48,49},{49,64},{64,6... | collective-permute-start | bytes 122888 | tf_op jit(solution)/shard_map/ppermute | solution.py:22
  17.7 37.6 %collective-permute-start.1 = (bf16[40,512]{1,0:T(8,128)(2,1)S(1)}, bf16[40,512]{1,0:T(8,128)(2,1)S(1)}, u32[]{:S(2)}, u32[]{:S(2)}) collective-permute-start(bf16[40,512]{1,0:T(8,128)(2,1)S(1)} %constant_dynamic-update-slice_fusion), channel_id=1, source_target_pairs={{1,0},{16,1},{17,16},{32,17},{33,32},{48,33},{49,48},{64,49},{65,6... | collective-permute-start | bytes 122888 | tf_op jit(solution)/shard_map/ppermute | solution.py:23
  55.4 0.8 fusion.34
  56.4 1.0 copy.42
  58.9 0.7 copy.44
  59.6 89.6 %all-gather.2.cloned.1.call-done = bf16[5120,1536]{1,0:T(8,128)(2,1)} async-done(((bf16[160,1536]{1,0:T(8,128)(2,1)}), bf16[5120,1536]{1,0:T(8,128)(2,1)}) %all-gather.2.cloned.1.call-update) | async-done | bytes 15728656 | tf_op jit(solution)/shard_map/all_gather | solution.py:144
  149.2 88.1 %while.21 = (s32[]{:T(128)}, f32[4,160]{1,0:T(4,128)S(1)}, f32[4,160]{1,0:T(4,128)S(1)}, f32[4,160,128]{2,1,0:T(8,128)S(1)}, f32[4,40]{1,0:T(4,128)S(1)}, /*inde...) while((s32[]{:T(128)}, f32[4,160]{1,0:T(4,128)S(1)}, ...), condition=%wide.region_5.6_spmd.clone, body=%wide.region_0.5_spmd.clone.sunk | while | flops 119781280 | bytes 9656456 | solution.py:114
  149.2 1.3 dynamic-slice_bitcast_fusion.2
  150.7 0.8 reshape.165
  152.5 1.3 fusion.62
  153.8 0.4 fusion.63
  154.7 1.3 dynamic-slice_bitcast_fusion.2
  156.2 0.8 reshape.165
  158.0 1.3 fusion.62
  159.4 0.4 fusion.63
  160.2 1.3 dynamic-slice_bitcast_fusion.2
  161.7 0.8 reshape.165
  163.5 1.3 fusion.62
  164.9 0.4 fusion.63
  165.7 1.3 dynamic-slice_bitcast_fusion.2
  167.2 0.8 reshape.165
  169.0 1.3 fusion.62
  171.3 1.3 dynamic-slice_bitcast_fusion.2
  172.7 0.8 reshape.165
  174.5 1.3 fusion.62
  176.8 1.3 dynamic-slice_bitcast_fusion.2
  178.2 0.8 reshape.165
  180.0 1.3 fusion.62
  182.3 1.3 dynamic-slice_bitcast_fusion.2
  183.7 0.8 reshape.165
  185.6 1.3 fusion.62
  187.8 1.3 dynamic-slice_bitcast_fusion.2
  189.2 0.8 reshape.165
  191.1 1.3 fusion.62
  193.3 1.3 dynamic-slice_bitcast_fusion.2
  194.8 0.8 reshape.165
  196.6 1.3 fusion.62
  198.8 1.3 dynamic-slice_bitcast_fusion.2
  200.3 0.8 reshape.165
  202.1 1.3 fusion.62
  203.4 0.4 fusion.63
  204.3 1.3 dynamic-slice_bitcast_fusion.2
  205.8 0.8 reshape.165
  207.6 1.3 fusion.62
  209.8 1.3 dynamic-slice_bitcast_fusion.2
  211.3 0.8 reshape.165
  213.1 1.3 fusion.62
  215.3 1.3 dynamic-slice_bitcast_fusion.2
  216.8 0.8 reshape.165
  218.6 1.3 fusion.62
  220.8 1.3 dynamic-slice_bitcast_fusion.2
  222.3 0.8 reshape.165
  224.1 1.3 fusion.62
  226.3 1.3 dynamic-slice_bitcast_fusion.2
  227.8 0.8 reshape.165
  229.6 1.3 fusion.62
  231.8 1.3 dynamic-slice_bitcast_fusion.2
  233.3 0.8 reshape.165
  235.1 1.3 fusion.62
  237.5 0.7 convert_element_type.38
  238.2 0.8 copy_bitcast_fusion
  (261 shorter events, 32.1 us)
Async XLA Ops:
  7.2 142.0 %all-gather.2.cloned.1.call-start = ((), (), s32[]{:S(2)}) async-start(), calls=%async_computation | async-start | bytes 16220160 | tf_op jit(solution)/shard_map/all_gather | solution.py:144
  10.7 46.8 %collective-permute-start = (bf16[40,512]{1,0:T(8,128)(2,1)S(1)}, bf16[40,512]{1,0:T(8,128)(2,1)S(1)}, u32[]{:S(2)}, u32[]{:S(2)}) collective-permute-start(bf16[40,512]{1,0:T(8,128)(2,1)S(1)} %constant_dynamic-update-slice_fusion), channel_id=1, source_target_pairs={{0,1},{1,16},{16,17},{17,32},{32,33},{33,48},{48,49},{49,64},{64,6... | collective-permute-start | bytes 122888 | tf_op jit(solution)/shard_map/ppermute | solution.py:22
  17.7 39.7 %collective-permute-start.1 = (bf16[40,512]{1,0:T(8,128)(2,1)S(1)}, bf16[40,512]{1,0:T(8,128)(2,1)S(1)}, u32[]{:S(2)}, u32[]{:S(2)}) collective-permute-start(bf16[40,512]{1,0:T(8,128)(2,1)S(1)} %constant_dynamic-update-slice_fusion), channel_id=1, source_target_pairs={{1,0},{16,1},{17,16},{32,17},{33,32},{48,33},{49,48},{64,49},{65,6... | collective-permute-start | bytes 122888 | tf_op jit(solution)/shard_map/ppermute | solution.py:23
Sparse Core Ops, SparseCore 0:
  10.1 139.0 all-gather.1
where the time goes:
time: 248 us; the launch traced here: 246 us
  waiting for transfers between devices  89.7 us (36%)
  local copies, waits for them, and re-layouts  44.9 us (18%)
  starting transfers between devices  44.7 us (18%)
  matrix products  36.4 us (15%)
  other arithmetic  14.5 us (6%)
  between operations  14.2 us (6%)
    all_gather x1, waiting for transfers between devices, body(): lax.all_gather(combined, ('seq', 'sub'), axis=0, tiled=True)  89.6 us
    ppermute x1, starting transfers between devices, with_halo(): lax.ppermute(leading, axis, [(b, a) for a, b in up])  37.6 us
    dot_general x33, matrix products, absorb(): jnp.einsum('qhe,khe->hqk', queries.reshape(query_count, head_count, head_...  25.7 us
    squeeze x16, local copies, waits for them, and re-layouts, fold_joint(): result, unused = lax.scan(one_block, states_in, blocks)  20.3 us
    reshape x16, local copies, waits for them, and re-layouts, absorb(): queries.reshape(query_count, head_count, head_size)  13.2 us
    dot_general x33, matrix products, absorb(): jnp.einsum('hqk,khe->hqe', weights.astype(jnp.bfloat16), value_rows.resha...  10.7 us
    reduce_sum x33, other arithmetic, absorb(): summed = summed * shrink + jnp.sum(weights, axis=2)  10.7 us
    ppermute x1, starting transfers between devices, with_halo(): lax.ppermute(last, axis, up)  7.05 us
  transfers between devices with their start and end apart: 3, of which 1 were waited for; matrix products, arithmetic and copies ran while one was open for 2% of the time, Pallas kernels for 0%

commit v1 on v0

--- a/solution.py
+++ b/solution.py
@@ -9,6 +9,13 @@
 AUDIO_DIM = 64
 TILE_LEN = 32
 STRETCH_LEN = 8
+
+
+def swapped_in(value, axis, d):
+    size = lax.axis_size(axis)
+    parts = jnp.stack([value for _ in range(size)])
+    parts = lax.all_to_all(parts, axis, split_axis=0, concat_axis=0)
+    return jnp.concatenate(parts, axis=d)
 
 
 def with_halo(array, sides, width):
@@ -141,7 +148,7 @@
         start_state(aud_q.shape[0], audio_heads, AUDIO_DIM),
     )
     video_state, audio_state = folder(
-        initial, lax.all_gather(combined, ("seq", "sub"), axis=0, tiled=True), jnp.int32(0)
+        initial, swapped_in(combined, ("seq", "sub"), 0), jnp.int32(0)
     )
     video_self = normalize_heads(video_state)
     audio_out = normalize_heads(audio_state)

time: 248 us -> 801 us (3.23)
  waiting for transfers between devices: 89.7 us -> 669 us
  matrix products: 36.4 us -> 21.8 us
  between operations: 14.2 us -> 0.89 us
  local copies, waits for them, and re-layouts: 44.9 us -> 35.8 us
    ppermute x1, waiting for transfers between devices: 0.01 us -> 649 us  [with_halo(): lax.ppermute(last, axis, up)]
    all_gather x1 -> x0, waiting for transfers between devices: 89.6 us -> none  [body(): lax.all_gather(combined, ('seq', 'sub'), axis=0, tiled=True)]
    all_to_all x0 -> x1, starting transfers between devices: none -> 46.5 us  [swapped_in(): parts = lax.all_to_all(parts, axis, split_axis=0, concat_axis=0)]
    ppermute x1, starting transfers between devices: 37.6 us -> 1.95 us  [with_halo(): lax.ppermute(leading, axis, [(b, a) for a, b in up])]
    ppermute x1, waiting for transfers between devices: 0.01 us -> 20.4 us  [with_halo(): lax.ppermute(leading, axis, [(b, a) for a, b in up])]
    dot_general x33, matrix products: 25.7 us -> 11.1 us  [absorb(): jnp.einsum('qhe,khe->hqk', queries.reshape(query_count, head_count, head_...]
    reshape x16, local copies, waits for them, and re-layouts: 13.2 us -> 1.5 us  [absorb(): queries.reshape(query_count, head_count, head_size)]
  transfers between devices with their start and end apart: 3 -> 3, of which waited for: 1 -> 2; matrix products, arithmetic and copies ran while one was open for 2% -> 0% of each run, Pallas kernels for 0% -> 0%
where the time goes in v1:
time: 801 us; the launch traced here: 795 us
  waiting for transfers between devices  669 us (84%)
  starting transfers between devices  52 us (6%)
  local copies, waits for them, and re-layouts  35.8 us (4%)
  matrix products  21.8 us (3%)
  other arithmetic  13.8 us (2%)
    ppermute x1, waiting for transfers between devices, with_halo(): lax.ppermute(last, axis, up)  649 us
    all_to_all x1, starting transfers between devices, swapped_in(): parts = lax.all_to_all(parts, axis, split_axis=0, concat_axis=0)  46.5 us
    ppermute x1, waiting for transfers between devices, with_halo(): lax.ppermute(leading, axis, [(b, a) for a, b in up])  20.4 us
    squeeze x16, local copies, waits for them, and re-layouts, fold_joint(): result, unused = lax.scan(one_block, states_in, blocks)  20.3 us
  transfers between devices with their start and end apart: 3, of which 2 were waited for; matrix products, arithmetic and copies ran while one was open for 0% of the time, Pallas kernels for 0%

profile of v1, /device:TPU:65, one launch (start us, length us, event | category | flops | bytes accessed | tf_op | source)
XLA Modules:
  0.0 795.1 jit_solution(2064035296084082592)
XLA Ops:
  0.6 1.1 pad_maximum_fusion
  1.7 5.7 stack.2
  7.5 46.5 %all-to-all-start = ((bf16[32,160,1536]{2,1,0:T(8,128)(2,1)}), bf16[32,160,1536]{2,1,0:T(8,128)(2,1)}, u32[]{:S(2)}, u32[]{:S(2)}) async-start(bf16[32,160,1536]{2,1,0:T(8,128)(2,1)} %stack.2), calls=%async_computation | async-start | bytes 31457280 | tf_op jit(solution)/shard_map/all_to_all | solution.py:17
  54.0 3.6 collective-permute-start
  57.6 2.0 collective-permute-start.1
  60.0 649.0 %collective-permute-done = bf16[40,512]{1,0:T(8,128)(2,1)S(1)} collective-permute-done((bf16[40,512]{1,0:T(8,128)(2,1)S(1)}, bf16[40,512]{1,0:T(8,128)(2,1)S(1)}, u32[]{:S(2)}, u32[]{:S(2)}) %collective-permute-start) | collective-permute-done | bytes 40992 | tf_op jit(solution)/shard_map/ppermute | solution.py:29
  709.0 20.4 %collective-permute-done.1 = bf16[40,512]{1,0:T(8,128)(2,1)S(1)} collective-permute-done((bf16[40,512]{1,0:T(8,128)(2,1)S(1)}, bf16[40,512]{1,0:T(8,128)(2,1)S(1)}, u32[]{:S(2)}, u32[]{:S(2)}) %collective-permute-start.1) | collective-permute-done | bytes 40992 | tf_op jit(solution)/shard_map/ppermute | solution.py:30
  729.7 0.4 fusion.35
  730.9 0.7 copy.44
  731.6 61.8 %while.21 = (s32[]{:T(128)}, f32[4,160]{1,0:T(4,128)S(1)}, f32[4,160]{1,0:T(4,128)S(1)}, f32[4,160,128]{2,1,0:T(8,128)S(1)}, f32[4,40]{1,0:T(4,128)S(1)}, /*inde...) while((s32[]{:T(128)}, f32[4,160]{1,0:T(4,128)S(1)}, ...), condition=%wide.region_5.6_spmd.clone, body=%wide.region_0.5_spmd.clone.sunk | while | flops 119781280 | bytes 9656456 | solution.py:121
  731.6 1.3 dynamic-slice_bitcast_fusion.2
  734.2 0.4 fusion.62
  734.6 0.4 fusion.63
  735.1 0.4 convolution_add_fusion.4
  735.5 1.3 dynamic-slice_bitcast_fusion.2
  738.1 0.4 fusion.62
  738.5 0.4 fusion.63
  738.9 0.4 convolution_add_fusion.4
  739.4 1.3 dynamic-slice_bitcast_fusion.2
  741.9 0.4 fusion.62
  742.3 0.4 fusion.63
  742.8 0.4 convolution_add_fusion.4
  743.2 1.3 dynamic-slice_bitcast_fusion.2
  745.8 0.4 fusion.62
  746.2 0.4 fusion.63
  746.7 0.4 convolution_add_fusion.4
  747.1 1.3 dynamic-slice_bitcast_fusion.2
  749.7 0.4 fusion.62
  750.1 0.4 fusion.63
  751.0 1.3 dynamic-slice_bitcast_fusion.2
  753.5 0.4 fusion.62
  753.9 0.4 fusion.63
  754.8 1.3 dynamic-slice_bitcast_fusion.2
  757.4 0.4 fusion.62
  757.8 0.4 fusion.63
  758.7 1.3 dynamic-slice_bitcast_fusion.2
  761.3 0.4 fusion.62
  761.7 0.4 fusion.63
  762.6 1.3 dynamic-slice_bitcast_fusion.2
  765.1 0.4 fusion.62
  765.5 0.4 fusion.63
  766.4 1.3 dynamic-slice_bitcast_fusion.2
  769.0 0.4 fusion.62
  769.4 0.4 fusion.63
  770.3 1.3 dynamic-slice_bitcast_fusion.2
  772.9 0.4 fusion.62
  773.3 0.4 fusion.63
  774.2 1.3 dynamic-slice_bitcast_fusion.2
  776.7 0.4 fusion.62
  777.1 0.4 fusion.63
  778.0 1.3 dynamic-slice_bitcast_fusion.2
  780.6 0.4 fusion.62
  781.0 0.4 fusion.63
  781.9 1.3 dynamic-slice_bitcast_fusion.2
  784.4 0.4 fusion.62
  784.9 0.4 fusion.63
  785.8 1.3 dynamic-slice_bitcast_fusion.2
  788.3 0.4 fusion.62
  788.7 0.4 fusion.63
  789.6 1.3 dynamic-slice_bitcast_fusion.2
  792.2 0.4 fusion.62
  792.6 0.4 fusion.63
  793.6 0.7 convert_element_type.38
  794.3 0.8 copy_bitcast_fusion
  (273 shorter events, 26.4 us)
Async XLA Ops:
  7.4 46.5 %copy-start.3 = (bf16[40,256]{1,0:T(8,128)(2,1)S(1)}, bf16[40,256]{1,0:T(8,128)(2,1)}, u32[]{:S(2)}) copy-start(bf16[40,256]{1,0:T(8,128)(2,1)} %param.19) | copy-start | bytes 61444
  7.4 46.5 %copy-start.4 = (bf16[40,256]{1,0:T(8,128)(2,1)S(1)}, bf16[40,256]{1,0:T(8,128)(2,1)}, u32[]{:S(2)}) copy-start(bf16[40,256]{1,0:T(8,128)(2,1)} %param.20) | copy-start | bytes 61444
  7.4 52.2 %copy-start.5 = (s32[2,160]{1,0:T(2,128)S(1)}, s32[2,160]{1,0:T(2,128)}, u32[]{:S(2)}) copy-start(s32[2,160]{1,0:T(2,128)} %param.21) | copy-start | bytes 3844
  7.5 52.5 %copy-start.2 = (bf16[160,256]{1,0:T(8,128)(2,1)S(1)}, bf16[160,256]{1,0:T(8,128)(2,1)}, u32[]{:S(2)}) copy-start(bf16[160,256]{1,0:T(8,128)(2,1)} %param.18) | copy-start | bytes 245764
  7.5 724.2 %copy-start = (bf16[160,512]{1,0:T(8,128)(2,1)S(1)}, bf16[160,512]{1,0:T(8,128)(2,1)}, u32[]{:S(2)}) copy-start(bf16[160,512]{1,0:T(8,128)(2,1)} %param.12) | copy-start | bytes 491524
  7.5 724.2 %copy-start.1 = (bf16[40,256]{1,0:T(8,128)(2,1)S(1)}, bf16[40,256]{1,0:T(8,128)(2,1)}, u32[]{:S(2)}) copy-start(bf16[40,256]{1,0:T(8,128)(2,1)} %param.15) | copy-start | bytes 61444
  7.5 724.1 %all-to-all-start = ((bf16[32,160,1536]{2,1,0:T(8,128)(2,1)}), bf16[32,160,1536]{2,1,0:T(8,128)(2,1)}, u32[]{:S(2)}, u32[]{:S(2)}) async-start(bf16[32,160,1536]{2,1,0:T(8,128)(2,1)} %stack.2), calls=%async_computation | async-start | bytes 31457280 | tf_op jit(solution)/shard_map/all_to_all | solution.py:17
  54.0 655.0 %collective-permute-start = (bf16[40,512]{1,0:T(8,128)(2,1)S(1)}, bf16[40,512]{1,0:T(8,128)(2,1)S(1)}, u32[]{:S(2)}, u32[]{:S(2)}) collective-permute-start(bf16[40,512]{1,0:T(8,128)(2,1)S(1)} %constant_dynamic-update-slice_fusion), channel_id=1, source_target_pairs={{0,1},{1,16},{16,17},{17,32},{32,33},{33,48},{48,49},{49,64},{64,6... | collective-permute-start | bytes 122888 | tf_op jit(solution)/shard_map/ppermute | solution.py:29
  57.6 671.8 %collective-permute-start.1 = (bf16[40,512]{1,0:T(8,128)(2,1)S(1)}, bf16[40,512]{1,0:T(8,128)(2,1)S(1)}, u32[]{:S(2)}, u32[]{:S(2)}) collective-permute-start(bf16[40,512]{1,0:T(8,128)(2,1)S(1)} %constant_dynamic-update-slice_fusion), channel_id=1, source_target_pairs={{1,0},{16,1},{17,16},{32,17},{33,32},{48,33},{49,48},{64,49},{65,6... | collective-permute-start | bytes 122888 | tf_op jit(solution)/shard_map/ppermute | solution.py:30
